TPU v7x, 16 devices: a whole 2x2x2 slice. The times are simulated.
16 devices in a mesh: fsdp: 16 (over z, y, x, core).
Axes of the slice: x: 2, y: 2, z: 2, core: 2. Of those that a mesh axis runs over, the one named last changes fastest.
Arguments:
- timesteps: float32 [8192], P('fsdp')
- guidance: float32 [8192], P('fsdp')
- pooled: bfloat16 [8192, 2048], P('fsdp')
- time_w1: bfloat16 [256, 1536], replicated
- time_b1: bfloat16 [1536], replicated
- time_w2: bfloat16 [1536, 1536], replicated
- time_b2: bfloat16 [1536], replicated
- guide_w1: bfloat16 [256, 1536], replicated
- guide_b1: bfloat16 [1536], replicated
- guide_w2: bfloat16 [1536, 1536], replicated
- guide_b2: bfloat16 [1536], replicated
- text_w1: bfloat16 [2048, 1536], replicated
- text_b1: bfloat16 [1536], replicated
- text_w2: bfloat16 [1536, 1536], replicated
- text_b2: bfloat16 [1536], replicated
- w_mod: bfloat16 [1536, 30720], P(None, 'fsdp')
- b_mod: bfloat16 [30720], P('fsdp')
- d_mods: bfloat16 [8192, 30720], P('fsdp')
Outputs:
- output 1: bfloat16 [8192, 30720], P('fsdp')
- output 2: float32 [1536, 30720], P(None, 'fsdp')
- output 3: float32 [30720], P('fsdp')
- output 4: float32 [256, 1536], replicated
- output 5: float32 [1536], replicated
- output 6: float32 [1536, 1536], replicated
- output 7: float32 [1536], replicated
- output 8: float32 [256, 1536], replicated
- output 9: float32 [1536], replicated
- output 10: float32 [1536, 1536], replicated
- output 11: float32 [1536], replicated
- output 12: float32 [2048, 1536], replicated
- output 13: float32 [1536], replicated
- output 14: float32 [1536, 1536], replicated
- output 15: float32 [1536], replicated
All inputs are finite; a program needn't handle non-finite values.
Results may differ from a plain program's by a relative error of at most 0.00492024.
Values are sent between devices in bfloat16 or wider.
A program may use at most 1 GiB of HBM per device.

v0:
```python
import math
import jax
import jax.numpy as jnp
from jax import lax
from jax.sharding import PartitionSpec as P

MESH_AXIS = "fsdp"
MAX_PERIOD = 10000.0
TIME_SCALE = 1000.0
CONTRACT_ROWS = (((0,), (0,)), ((), ()))
CONTRACT_COLS = (((1,), (1,)), ((), ()))


def sinusoid(values, freq_width):
    half_width = freq_width // 2
    freq_table = jnp.exp(-math.log(MAX_PERIOD) * jnp.arange(half_width, dtype=jnp.float32) / half_width)
    angles = (TIME_SCALE * values)[:, None] * freq_table[None, :]
    return jnp.concatenate([jnp.cos(angles), jnp.sin(angles)], axis=1).astype(jnp.bfloat16)


def silu_grad(values):
    sigmoid_v = jax.nn.sigmoid(values)
    return sigmoid_v * (1.0 + values * (1.0 - sigmoid_v))


def mlp_forward(inputs_bf, params):
    hidden = jnp.dot(inputs_bf, params[0], preferred_element_type=jnp.float32) + params[1].astype(jnp.float32)
    act_bf = jax.nn.silu(hidden).astype(jnp.bfloat16)
    output = jnp.dot(act_bf, params[2], preferred_element_type=jnp.float32) + params[3].astype(jnp.float32)
    return output, hidden, act_bf


def mlp_backward(inputs_bf, params, hidden, act_bf, d_out, d_out_bf):
    grad_w2 = lax.dot_general(act_bf, d_out_bf, CONTRACT_ROWS, preferred_element_type=jnp.float32)
    grad_b2 = jnp.sum(d_out, axis=0)
    d_act = lax.dot_general(d_out_bf, params[2], CONTRACT_COLS, preferred_element_type=jnp.float32)
    d_hidden = d_act * silu_grad(hidden)
    grad_w1 = lax.dot_general(inputs_bf, d_hidden.astype(jnp.bfloat16), CONTRACT_ROWS, preferred_element_type=jnp.float32)
    grad_b1 = jnp.sum(d_hidden, axis=0)
    return (grad_w1, grad_b1, grad_w2, grad_b2)


def embed_forward(inputs_list, params_list):
    saved_acts = [mlp_forward(inputs_bf, params) for inputs_bf, params in zip(inputs_list, params_list)]
    cond_vec = saved_acts[0][0] + saved_acts[1][0] + saved_acts[2][0]
    return cond_vec, saved_acts


def embed_backward(inputs_list, params_list, saved_acts, d_vec):
    d_vec_bf = d_vec.astype(jnp.bfloat16)
    grad_list = []
    for inputs_bf, params, record in zip(inputs_list, params_list, saved_acts):
        grad_list.extend(mlp_backward(inputs_bf, params, record[1], record[2], d_vec, d_vec_bf))
    return tuple(grad_list)


def solution(mesh):
    row_split = P(MESH_AXIS)
    row_matrix = P(MESH_AXIS, None)
    col_matrix = P(None, MESH_AXIS)
    embed_specs = (P(None, None), P(None), P(None, None), P(None)) * 3
    in_specs = (row_split, row_split, row_matrix) + embed_specs + (col_matrix, row_split, row_matrix)
    out_specs = (row_matrix, col_matrix, row_split) + embed_specs

    def local_step(timesteps, guidance, pooled, time_w1, time_b1, time_w2, time_b2, guide_w1, guide_b1, guide_w2, guide_b2, text_w1, text_b1, text_w2, text_b2, w_mod, b_mod, d_mods):
        freq_width = time_w1.shape[0]
        inputs_list = [sinusoid(timesteps, freq_width), sinusoid(guidance, freq_width), pooled]
        params_list = [(time_w1, time_b1, time_w2, time_b2), (guide_w1, guide_b1, guide_w2, guide_b2), (text_w1, text_b1, text_w2, text_b2)]
        cond_vec, saved_acts = embed_forward(inputs_list, params_list)
        cond_silu = jax.nn.silu(cond_vec).astype(jnp.bfloat16)
        full_wmod = lax.all_gather(w_mod, MESH_AXIS, axis=1, tiled=True)
        full_bmod = lax.all_gather(b_mod, MESH_AXIS, axis=0, tiled=True)
        modulation = (jnp.dot(cond_silu, full_wmod, preferred_element_type=jnp.float32) + full_bmod.astype(jnp.float32)).astype(jnp.bfloat16)
        part_wgrad = lax.dot_general(cond_silu, d_mods, CONTRACT_ROWS, preferred_element_type=jnp.float32)
        grad_wmod = lax.psum_scatter(part_wgrad, MESH_AXIS, scatter_dimension=1, tiled=True)
        part_bgrad = jnp.sum(d_mods, axis=0, dtype=jnp.float32)
        grad_bmod = lax.psum_scatter(part_bgrad, MESH_AXIS, scatter_dimension=0, tiled=True)
        d_cond = lax.dot_general(d_mods, full_wmod, CONTRACT_COLS, preferred_element_type=jnp.float32)
        d_vec = d_cond * silu_grad(cond_vec)
        embed_grads = lax.psum(embed_backward(inputs_list, params_list, saved_acts, d_vec), MESH_AXIS)
        return (modulation, grad_wmod, grad_bmod) + tuple(embed_grads)

    return jax.shard_map(local_step, mesh=mesh, in_specs=in_specs, out_specs=out_specs, check_vma=False)
```

profile of v0, /device:TPU:0, one launch (start us, length us, event | category | flops | bytes accessed | tf_op | source)
XLA Modules:
  0.0 1750.3 jit_solution(15341765722035819870)
XLA Ops:
  7.2 0.0 copy-start
  7.3 0.0 all-gather.3.cloned.1.call-start
  7.3 0.7 all-gather.3.cloned.1.call-update
  8.0 0.0 all-reduce.5.cloned.1.call-start
  8.1 0.0 copy-done.26
  8.3 2.2 fusion.9
  10.5 0.0 copy-start.12
  10.5 0.0 copy-start.8
  10.5 0.0 copy-start.10
  10.5 0.0 copy-start.14
  10.6 0.0 copy-start.32
  10.6 0.6 convolution_add_fusion
  11.1 0.0 copy-start.2
  11.2 0.0 copy-done.8
  11.2 0.0 copy-done.10
  11.2 0.0 copy-done.14
  11.3 0.0 copy-done.17
  11.3 0.6 convolution_add_fusion.1
  11.9 2.8 copy-done.32
  14.6 3.4 convolution_add_fusion.3
  18.1 0.0 copy-start.33
  18.1 0.0 slice-start.6
  18.1 0.0 slice-start.4
  18.1 2.7 convolution_add_fusion.5
  20.8 0.0 copy-done.2
  20.8 0.0 slice-done.5
  20.8 0.0 slice-done.6
  20.8 2.6 fusion.1
  23.5 4.3 fusion
  27.8 11.3 convert_reduce_fusion
  39.1 303.4 %all-gather.3.cloned.1.call-done = bf16[1536,30720]{1,0:T(8,128)(2,1)} async-done(((bf16[1536,1920]{1,0:T(8,128)(2,1)}), bf16[1536,30720]{1,0:T(8,128)(2,1)}) %all-gather.3.cloned.1.call-update) | async-done | bytes 94371856 | tf_op jit(solution)/shard_map/all_gather | solution.py:71
  342.5 62.3 %fusion.19 = (f32[1536]{0:T(1024)}, bf16[512,1536]{1,0:T(8,128)(2,1)}) fusion(f32[512,1536]{1,0:T(8,128)} %fusion, bf16[512,30720]{1,0:T(8,128)(2,1)} %param.35, bf16[1536,30720]{1,0:T(8,128)(2,1)} %all-gather.3.cloned.1.call-done), kind=kOutput, calls=%fused_computation.49 | convolution fusion | flops 48326246400 | bytes 130553856 | tf_op jit(solution)/shard_map/dot_general | solution.py:78
  404.8 7.7 fusion.22
  412.5 6.3 fusion.21
  418.8 3.8 fusion.20
  422.7 5.4 fusion.15
  428.1 5.2 fusion.16
  433.3 5.2 fusion.17
  438.5 1.7 fusion.3
  440.2 1.7 fusion.5
  442.0 6.6 convolution_bitcast_fusion
  448.6 0.0 all-reduce.5.cloned.1.call-update
  448.6 0.0 reduce-scatter.2.cloned.1.call-start
  448.7 79.9 %fusion.18 = f32[1536,30720]{1,0:T(8,128)} fusion(bf16[512,30720]{1,0:T(8,128)(2,1)} %param.35, f32[512,1536]{1,0:T(8,128)} %fusion), kind=kOutput, calls=%fused_computation.48 | convolution fusion | flops 48322314240 | bytes 223346688 | tf_op jit(solution)/shard_map/dot_general | solution.py:74
  528.5 0.0 copy-start.21
  528.6 0.0 copy-start.22
  528.6 0.0 reduce-scatter.2.cloned.1.call-update
  528.6 0.6 copy-done.29
  529.2 13.6 all-gather
  542.8 0.1 convert_element_type.70
  543.0 33.1 %all-reduce.1 = (f32[1536]{0:T(1024)}, f32[1536]{0:T(1024)S(1)}, f32[1536]{0:T(1024)}, f32[1536]{0:T(1024)}) all-reduce(f32[1536]{0:T(1024)S(1)} %copy-done.22, f32[1536]{0:T(1024)S(1)} %copy-done.19, f32[1536]{0:T(1024)S(1)} %copy-done.21, f32[1536]{0:T(1024)S(1)} %copy-done.20), channel_id=1, replica_groups=mesh['fsdp'=16] {'fsdp'}, use_global_device_ids=true, to_apply=%region_5.6 | all-reduce | flops 6144 | bytes 49152 | tf_op jit(solution)/shard_map/psum | solution.py:80
  576.1 58.8 %add_convert_fusion = bf16[512,30720]{1,0:T(8,128)(2,1)} fusion(bf16[1536,30720]{1,0:T(8,128)(2,1)} %all-gather.3.cloned.1.call-done, f32[30720]{0:T(1024)S(1)} %bitcast.31, f32[512,1536]{1,0:T(8,128)} %fusion), kind=kOutput, calls=%fused_computation.1 | convolution fusion | flops 48353771520 | bytes 129097728 | tf_op jit(solution)/shard_map/dot_general | solution.py:73
  635.0 217.3 %all-reduce.5.cloned.1.call-done = (f32[30720]{0:T(1024)}, f32[256,1536]{1,0:T(8,128)}, f32[1536,1536]{1,0:T(8,128)}, f32[256,1536]{1,0:T(8,128)}, f32[1536,1536...) async-done(((f32[30720]{0:T(1024)}, f32[256,1536]{1,0:T(8,128)}, f32[1536,1536]{1,0:T(8,128)}, f32[256,1536]{1,0:T(8,128)}, f32[1536,1536]{1,0:T(8,128)}, ...) | async-done | bytes 44163088
  852.2 12.7 copy.34
  865.0 1.4 dynamic-slice
  866.3 852.2 %reduce-scatter.2.cloned.1.call-done = f32[1536,1920]{1,0:T(8,128)} async-done(((f32[1536,30720]{1,0:T(8,128)}), f32[1536,1920]{1,0:T(8,128)}) %reduce-scatter.2.cloned.1.call-update) | async-done | bytes 11796496 | tf_op jit(solution)/shard_map/reduce_scatter | solution.py:75
  1718.6 0.6 copy.44
  1719.2 0.6 copy.45
  1719.8 1.1 copy.46
  1720.9 8.4 copy.47
  1729.3 1.1 copy.48
  1730.4 9.0 copy.49
  1739.4 0.0 copy-start.1
  1739.4 3.9 copy.50
  (85 shorter events, 0.2 us)
Async XLA Ops:
  7.2 4.7 copy-start
  7.2 0.9 copy-start.23
  7.2 0.9 copy-start.24
  7.2 0.9 copy-start.25
  7.2 0.9 copy-start.26
  7.2 0.9 copy-start.27
  7.3 0.9 copy-start.28
  7.3 1.0 copy-start.30
  7.3 1.0 copy-start.31
  7.3 3.3 copy-start.16
  7.3 335.2 %all-gather.3.cloned.1.call-start = ((), (), s32[]{:S(2)}) async-start(), calls=%async_computation.1 | async-start | bytes 100270080 | tf_op jit(solution)/shard_map/all_gather | solution.py:71
  8.0 844.2 %all-reduce.5.cloned.1.call-start = ((), (), s32[]{:S(2)}) async-start(), calls=%async_computation.3 | async-start | bytes 88326144
  8.1 3.2 copy-start.17
  10.5 0.7 copy-start.12
  10.5 0.7 copy-start.8
  10.5 0.7 copy-start.10
  10.5 0.7 copy-start.14
  10.6 4.1 copy-start.32
  11.1 9.6 copy-start.2
  11.3 6.8 slice-start.7
  14.6 3.4 copy-start.4
  14.6 3.4 slice-start.8
  14.6 6.2 slice-start.5
  14.6 8.8 slice-start.3
  18.1 5.4 copy-start.33
  18.1 2.7 slice-start.6
  18.1 5.4 slice-start.4
  404.8 7.7 copy-start.3
  404.8 7.7 copy-start.35
  404.8 14.0 slice-start.9
  412.5 6.3 copy-start.5
  412.5 6.3 slice-start.10
  428.1 5.2 copy-start.34
  433.3 5.2 copy-start.13
  433.3 5.2 copy-start.15
  438.5 1.8 copy-start.9
  438.5 1.8 copy-start.11
  448.6 1269.9 %reduce-scatter.2.cloned.1.call-start = ((), (), s32[]{:S(2)}) async-start(), calls=%async_computation.2 | async-start | bytes 200540160 | tf_op jit(solution)/shard_map/reduce_scatter | solution.py:75
  528.5 0.7 copy-start.29
  528.5 14.4 copy-start.19
  528.5 14.4 copy-start.20
  528.5 14.4 copy-start.21
  528.6 14.4 copy-start.22
  576.1 1143.0 %copy-start.18 = (f32[1536]{0:T(1024)}, f32[1536]{0:T(1024)S(1)}, u32[]{:S(2)}) copy-start(f32[1536]{0:T(1024)S(1)} %get-tuple-element.115) | copy-start | bytes 18436
  852.2 867.5 %copy-start.7 = (f32[256,1536]{1,0:T(8,128)S(1)}, f32[256,1536]{1,0:T(8,128)}, u32[]{:S(2)}) copy-start(f32[256,1536]{1,0:T(8,128)} %get-tuple-element.112) | copy-start | bytes 4718596
  1720.9 8.4 copy-start.6
  1729.3 10.1 slice-start
  1730.4 9.0 slice-start.1
  1730.4 9.0 slice-start.2
  1739.4 3.9 copy-start.1
Sparse Core Ops, SparseCore 0:
  10.4 332.1 all-gather.2
  448.7 403.4 all-reduce.4
  858.0 860.4 reduce-scatter.1
where the time goes:
time: 1760 us; the launch traced here: 1750 us
  waiting for transfers between devices  1370 us (78%)
  matrix products  259 us (15%)
  blocking collectives  46.7 us (3%)
  local copies, waits for them, and re-layouts  42.5 us (2%)
    reduce_scatter x1, waiting for transfers between devices, local_step(): lax.psum_scatter(part_wgrad, MESH_AXIS, scatter_dimension=1, tiled=True)  852 us
    all_gather x1, waiting for transfers between devices, local_step(): full_wmod = lax.all_gather(w_mod, MESH_AXIS, axis=1, tiled=True)  303 us
    unnamed x4, waiting for transfers between devices  218 us
    dot_general x1, matrix products, local_step(): lax.dot_general(cond_silu, d_mods, CONTRACT_ROWS, preferred_element_type=...  79.9 us
    dot_general x1, matrix products, local_step(): lax.dot_general(d_mods, full_wmod, CONTRACT_COLS, preferred_element_type=...  62.3 us
    dot_general x1, matrix products, local_step(): jnp.dot(cond_silu, full_wmod, preferred_element_type=jnp.float32)  58.8 us
    unnamed x104, local copies, waits for them, and re-layouts  42.5 us
  transfers between devices with their start and end apart: 3, of which 3 were waited for; matrix products, arithmetic and copies ran while one was open for 10% of the time, Pallas kernels for 0%

commit v1 on v0

v1 whole, which is shorter than its diff:
```python
import math
import jax
import jax.numpy as jnp
from jax import lax
from jax.experimental import pallas as pl
from jax.experimental.pallas import tpu as pltpu
from jax.sharding import PartitionSpec as P

MESH_AXIS = "fsdp"
MAX_PERIOD = 10000.0
TIME_SCALE = 1000.0
CONTRACT_ROWS = (((0,), (0,)), ((), ()))
CONTRACT_COLS = (((1,), (1,)), ((), ()))
COLOURS = ((2, 4, 8), (4, 8, 2), (8, 2, 4))
G_GROUPS = ((2, 3, 4, 5, 8, 9), (6, 7, 10, 11, 12, 13), (14, 15))
CALLS = ((0, 1), (2, 3), (4, 5), (6,), (7,))
ROUNDS = (((), 0), ((), 1), ((), 2), ((0,), 1), ((0,), 2), ((1,), 2), ((0, 1), 2))
VMEM_LIMIT = 60 * 1024 * 1024


def sinusoid(values, freq_width):
    half_width = freq_width // 2
    freq_table = jnp.exp(-math.log(MAX_PERIOD) * jnp.arange(half_width, dtype=jnp.float32) / half_width)
    angles = (TIME_SCALE * values)[:, None] * freq_table[None, :]
    return jnp.concatenate([jnp.cos(angles), jnp.sin(angles)], axis=1).astype(jnp.bfloat16)


def silu_grad(values):
    sigmoid_v = jax.nn.sigmoid(values)
    return sigmoid_v * (1.0 + values * (1.0 - sigmoid_v))


def mlp_forward(inputs_bf, params):
    hidden = jnp.dot(inputs_bf, params[0], preferred_element_type=jnp.float32) + params[1].astype(jnp.float32)
    act_bf = jax.nn.silu(hidden).astype(jnp.bfloat16)
    return jnp.dot(act_bf, params[2], preferred_element_type=jnp.float32) + params[3].astype(jnp.float32)


def cost(flops, bytes_accessed):
    return pl.CostEstimate(flops=flops, bytes_accessed=bytes_accessed, transcendentals=0)


def dot_f32(a, b, dims):
    return lax.dot_general(a, b, dims, preferred_element_type=jnp.float32)


def split_for_partner(core, d_mods, n_dev, cols):
    rows = d_mods.shape[0]

    def body(core_ref, src_ref, dst_ref):
        dst_ref[0] = src_ref[...]

    return pl.pallas_call(
        body,
        name="split_for_partner",
        grid_spec=pltpu.PrefetchScalarGridSpec(
            num_scalar_prefetch=1,
            grid=(n_dev // 2,),
            in_specs=[pl.BlockSpec((rows, cols), lambda j, c: (0, 2 * j + 1 - c[0]))],
            out_specs=pl.BlockSpec((1, rows, cols), lambda j, c: (j, 0, 0)),
        ),
        out_shape=jax.ShapeDtypeStruct((n_dev // 2, rows, cols), d_mods.dtype),
        cost_estimate=cost(n_dev * rows * cols, 2 * n_dev * rows * cols),
    )(core, d_mods)


def place_blocks(core, modulation, blocks):
    chips, rows, cols = blocks.shape

    def body(core_ref, src_ref, old_ref, dst_ref):
        dst_ref[...] = src_ref[0]

    return pl.pallas_call(
        body,
        name="place_blocks",
        grid_spec=pltpu.PrefetchScalarGridSpec(
            num_scalar_prefetch=1,
            grid=(chips,),
            in_specs=[pl.BlockSpec((1, rows, cols), lambda j, c: (j, 0, 0)), pl.BlockSpec(memory_space=pl.ANY)],
            out_specs=pl.BlockSpec((rows, cols), lambda j, c: (0, 2 * j + 1 - c[0])),
        ),
        out_shape=jax.ShapeDtypeStruct(modulation.shape, modulation.dtype),
        input_output_aliases={2: 0},
        cost_estimate=cost(2 * chips * rows * cols, 4 * chips * rows * cols),
    )(core, blocks, modulation)


def column_rounds(where, s_own, s_their, g_own, g_their, bias, w_blocks, carry):
    n = len(w_blocks)
    hidden, width = w_blocks[0].shape
    rows = s_own.shape[0]
    chips, _, cols = g_their.shape
    total = g_own.shape[1]
    first = carry is None

    def body(where_ref, so_ref, st_ref, go_ref, gt_ref, b_ref, *refs):
        w_refs, refs = refs[:n], refs[n:]
        if not first:
            old_ref, refs = refs[0], refs[3:]
        mo_ref, mt_ref, dc_ref = refs
        step = pl.program_id(0)

        @pl.when(step == 0)
        def _():
            dc_ref[...] = jnp.zeros_like(dc_ref) if first else old_ref[...]

        for k in range(n):
            @pl.when(step == k)
            def _(k=k):
                w = w_refs[k][...]
                dc_ref[:rows] += dot_f32(go_ref[...], w, CONTRACT_COLS)
                dc_ref[rows:] += dot_f32(gt_ref[0], w, CONTRACT_COLS)
                mo_ref[...] = (jnp.dot(so_ref[...], w, preferred_element_type=jnp.float32) + b_ref[...]).astype(mo_ref.dtype)
                mt_ref[0] = (jnp.dot(st_ref[...], w, preferred_element_type=jnp.float32) + b_ref[...]).astype(mt_ref.dtype)

    def own_col(k, w):
        return 0, w[k]

    def their_col(k, w):
        return w[n + k], 0, w[2 * n + k]

    fixed = lambda k, w: (0, 0)
    once = pl.Buffered(1)
    in_specs = [pl.BlockSpec((rows, hidden), fixed, pipeline_mode=once)] * 2
    in_specs += [pl.BlockSpec((rows, width), own_col), pl.BlockSpec((1, rows, width), their_col), pl.BlockSpec((1, width), own_col)]
    in_specs += [pl.BlockSpec((hidden, width), fixed, pipeline_mode=once)] * n
    operands = [s_own, s_their, g_own, g_their, bias, *w_blocks]
    aliases = {}
    if not first:
        in_specs += [pl.BlockSpec((2 * rows, hidden), fixed, pipeline_mode=once), pl.BlockSpec(memory_space=pl.ANY), pl.BlockSpec(memory_space=pl.ANY)]
        operands += [carry[2], carry[0], carry[1]]
        base = 1 + 5 + n
        aliases = {base: 2, base + 1: 0, base + 2: 1}
    return pl.pallas_call(
        body,
        name="column_rounds",
        grid_spec=pltpu.PrefetchScalarGridSpec(
            num_scalar_prefetch=1,
            grid=(n,),
            in_specs=in_specs,
            out_specs=[pl.BlockSpec((rows, width), own_col), pl.BlockSpec((1, rows, width), their_col), pl.BlockSpec((2 * rows, hidden), fixed)],
        ),
        out_shape=[jax.ShapeDtypeStruct((rows, total), jnp.bfloat16), jax.ShapeDtypeStruct((chips, rows, cols), jnp.bfloat16), jax.ShapeDtypeStruct((2 * rows, hidden), jnp.float32)],
        input_output_aliases=aliases,
        cost_estimate=cost(8 * n * rows * hidden * width, 2 * n * hidden * width + 8 * n * rows * width),
        compiler_params=pltpu.CompilerParams(vmem_limit_bytes=VMEM_LIMIT),
    )(where, *operands)


def sum_silu(core, part_cond, incoming, bias):
    batch, hidden = part_cond.shape
    block = 512
    steps = batch // 2 // block

    def body(core_ref, a_ref, b_ref, bias_ref, out_ref):
        value = a_ref[...] + b_ref[...] + bias_ref[...]
        out_ref[...] = (value * jax.nn.sigmoid(value)).astype(jnp.bfloat16).T

    return pl.pallas_call(
        body,
        name="sum_silu",
        grid_spec=pltpu.PrefetchScalarGridSpec(
            num_scalar_prefetch=1,
            grid=(steps,),
            in_specs=[pl.BlockSpec((block, hidden), lambda i, c: (i + c[0] * steps, 0)), pl.BlockSpec((block, hidden), lambda i, c: (i, 0)), pl.BlockSpec((1, hidden), lambda i, c: (0, 0))],
            out_specs=pl.BlockSpec((hidden, block), lambda i, c: (0, i)),
        ),
        out_shape=jax.ShapeDtypeStruct((hidden, batch // 2), jnp.bfloat16),
        cost_estimate=cost(4 * batch * hidden, 10 * batch // 2 * hidden),
        compiler_params=pltpu.CompilerParams(vmem_limit_bytes=VMEM_LIMIT),
    )(core, part_cond, incoming, bias)


def embed_body(core_ref, t_ref, g_ref, u_ref, wt1, wg1, wu1, bt1, bg1, bu1, wt2, wg2, wu2, h_ref, c_ref):
    total = None
    for k, (x_ref, w1, b1, w2) in enumerate(((t_ref, wt1, bt1, wt2), (g_ref, wg1, bg1, wg2), (u_ref, wu1, bu1, wu2))):
        hidden = jnp.dot(x_ref[...], w1[...], preferred_element_type=jnp.float32) + b1[...]
        h_ref[k] = hidden
        act = (hidden * jax.nn.sigmoid(hidden)).astype(jnp.bfloat16)
        part = jnp.dot(act, w2[...], preferred_element_type=jnp.float32)
        total = part if total is None else total + part
    c_ref[...] = total


def embed_half(core, inputs_list, params_list, block):
    batch = inputs_list[0].shape[0]
    hidden, out_width = params_list[0][2].shape
    half = hidden // 2
    rows = [pl.BlockSpec((block, x.shape[1]), lambda i, c: (i, 0)) for x in inputs_list]
    firsts = [pl.BlockSpec((p[0].shape[0], half), lambda i, c: (0, c[0])) for p in params_list]
    biases = [pl.BlockSpec((1, half), lambda i, c: (0, c[0])) for p in params_list]
    seconds = [pl.BlockSpec((half, out_width), lambda i, c: (c[0], 0)) for p in params_list]
    flops = sum(2 * batch * half * (p[0].shape[0] + out_width) for p in params_list)
    return pl.pallas_call(
        embed_body,
        name="embed_half",
        grid_spec=pltpu.PrefetchScalarGridSpec(
            num_scalar_prefetch=1,
            grid=(batch // block,),
            in_specs=rows + firsts + biases + seconds,
            out_specs=[pl.BlockSpec((3, block, half), lambda i, c: (0, i, 0)), pl.BlockSpec((block, out_width), lambda i, c: (i, 0))],
        ),
        out_shape=[jax.ShapeDtypeStruct((3, batch, half), jnp.float32), jax.ShapeDtypeStruct((batch, out_width), jnp.float32)],
        cost_estimate=cost(flops, 4 * batch * (3 * half + out_width)),
        compiler_params=pltpu.CompilerParams(vmem_limit_bytes=VMEM_LIMIT),
    )(core, *inputs_list, *(p[0] for p in params_list), *(p[1].astype(jnp.float32)[None] for p in params_list), *(p[2] for p in params_list))


def embed_grad_body(n_mlp, *refs):
    d_ref, refs = refs[0], refs[1:]
    x_refs, h_refs, w2_refs, outs = refs[:n_mlp], refs[n_mlp:2 * n_mlp], refs[2 * n_mlp:3 * n_mlp], refs[3 * n_mlp:]

    @pl.when(pl.program_id(0) == 0)
    def _():
        for out in outs:
            out[...] = jnp.zeros_like(out)

    for k in range(n_mlp):
        g1_ref, b1_ref, g2_ref = outs[3 * k:3 * k + 3]
        hidden = h_refs[k][0]
        sig = jax.nn.sigmoid(hidden)
        act = (hidden * sig).astype(jnp.bfloat16)
        d_act = dot_f32(d_ref[...], w2_refs[k][...], CONTRACT_COLS)
        d_hidden = d_act * (sig * (1.0 + hidden * (1.0 - sig)))
        b1_ref[...] += jnp.sum(d_hidden, axis=0, keepdims=True)
        g2_ref[...] += dot_f32(act, d_ref[...], CONTRACT_ROWS)
        g1_ref[...] += dot_f32(x_refs[k][...], d_hidden.astype(jnp.bfloat16), CONTRACT_ROWS)


def embed_grad(core, d_vec_all, which, inputs_list, hidden_all, params_list, block):
    batch, out_width = d_vec_all.shape
    half = hidden_all.shape[2]
    n_mlp = len(which)

    def body(core_ref, *refs):
        embed_grad_body(n_mlp, *refs)

    in_specs = [pl.BlockSpec((block, out_width), lambda i, c: (i, 0))]
    in_specs += [pl.BlockSpec((block, inputs_list[k].shape[1]), lambda i, c: (i, 0)) for k in which]
    in_specs += [pl.BlockSpec((1, block, half), lambda i, c, k=k: (k, i, 0)) for k in which]
    in_specs += [pl.BlockSpec((half, out_width), lambda i, c: (c[0], 0)) for k in which]
    shapes = [s for k in which for s in ((inputs_list[k].shape[1], half), (1, half), (half, out_width))]
    flops = sum(2 * batch * half * (2 * out_width + inputs_list[k].shape[1]) for k in which)
    return pl.pallas_call(
        body,
        name="embed_grad",
        grid_spec=pltpu.PrefetchScalarGridSpec(
            num_scalar_prefetch=1,
            grid=(batch // block,),
            in_specs=in_specs,
            out_specs=[pl.BlockSpec(s, lambda i, c: (0, 0)) for s in shapes],
        ),
        out_shape=[jax.ShapeDtypeStruct(s, jnp.float32) for s in shapes],
        cost_estimate=cost(flops, 2 * batch * (out_width + 4 * half)),
        compiler_params=pltpu.CompilerParams(vmem_limit_bytes=VMEM_LIMIT),
    )(core, d_vec_all, *(inputs_list[k] for k in which), *([hidden_all] * n_mlp), *(params_list[k][2] for k in which))


def mod_weight_grad(where, mine_t, theirs_t, blocks, width, carry):
    n = len(blocks)
    hidden = mine_t.shape[0]
    rows = blocks[0][0].shape[0]
    cols = width
    tile = cols // 3
    first = carry is None

    def body(where_ref, mine_ref, theirs_ref, *refs):
        g_refs, refs = refs[:n], refs[n:]
        if not first:
            old_w, old_b, refs = refs[0], refs[1], refs[2:]
        w_ref, b_ref = refs
        step = pl.program_id(1)

        @pl.when(step == 0)
        def _():
            w_ref[...] = jnp.zeros_like(w_ref) if first else old_w[...]
            b_ref[...] = jnp.zeros_like(b_ref) if first else old_b[...]

        for k in range(n):
            @pl.when(step == k)
            def _(k=k):
                block = g_refs[k][...]
                b_ref[...] += jnp.sum(block.astype(jnp.float32), axis=0, keepdims=True)

                @pl.when(where_ref[n + k] == 1)
                def _():
                    w_ref[...] += jnp.dot(mine_ref[...], block, preferred_element_type=jnp.float32)

                @pl.when(where_ref[n + k] == 0)
                def _():
                    w_ref[...] += jnp.dot(theirs_ref[...], block, preferred_element_type=jnp.float32)

    def mine_map(t, k, w):
        return 0, jnp.where(w[n + k] == 1, w[k], 0)

    def theirs_map(t, k, w):
        return 0, jnp.where(w[n + k] == 1, 0, w[k])

    in_specs = [pl.BlockSpec((hidden, rows), mine_map), pl.BlockSpec((hidden, rows), theirs_map)]
    operands = [mine_t, theirs_t]
    for array, own in blocks:
        in_specs.append(pl.BlockSpec((rows, tile), (lambda t, k, w: (0, 3 * w[2 * n] + t)) if own else (lambda t, k, w: (0, t))))
        operands.append(array)
    out_specs = [pl.BlockSpec((hidden, tile), lambda t, k, w: (0, t)), pl.BlockSpec((1, tile), lambda t, k, w: (0, t))]
    aliases = {}
    if not first:
        in_specs += out_specs
        operands += list(carry)
        aliases = {3 + n: 0, 4 + n: 1}
    return pl.pallas_call(
        body,
        name="mod_weight_grad",
        grid_spec=pltpu.PrefetchScalarGridSpec(num_scalar_prefetch=1, grid=(3, n), in_specs=in_specs, out_specs=out_specs),
        out_shape=[jax.ShapeDtypeStruct((hidden, cols), jnp.float32), jax.ShapeDtypeStruct((1, cols), jnp.float32)],
        input_output_aliases=aliases,
        cost_estimate=cost(2 * n * rows * hidden * cols, 2 * n * rows * (3 * hidden + cols) + 8 * hidden * cols),
        compiler_params=pltpu.CompilerParams(vmem_limit_bytes=VMEM_LIMIT),
    )(where, *operands)


def join_halves(core, mine, theirs, axis):
    shape = list(mine.shape)
    shape[axis] *= 2
    block = mine.shape

    def body(core_ref, mine_ref, theirs_ref, out_ref):
        is_mine = pl.program_id(0) == core_ref[0]

        @pl.when(is_mine)
        def _():
            out_ref[...] = mine_ref[...]

        @pl.when(jnp.logical_not(is_mine))
        def _():
            out_ref[...] = theirs_ref[...]

    steps = 4 if block[1 - axis] % 32 == 0 else 1
    if axis == 0:
        part = (block[0], block[1] // steps)
        whole_map = lambda h, i, c: (h, i)
        part_map = lambda h, i, c: (0, i)
    else:
        part = (block[0] // steps, block[1])
        whole_map = lambda h, i, c: (i, h)
        part_map = lambda h, i, c: (i, 0)
    size = shape[0] * shape[1]
    return pl.pallas_call(
        body,
        name="join_halves",
        grid_spec=pltpu.PrefetchScalarGridSpec(
            num_scalar_prefetch=1,
            grid=(2, steps),
            in_specs=[pl.BlockSpec(part, part_map)] * 2,
            out_specs=pl.BlockSpec(part, whole_map),
        ),
        out_shape=jax.ShapeDtypeStruct(shape, jnp.float32),
        cost_estimate=cost(4 * size, 8 * size),
    )(core, mine, theirs)


def solution(mesh):
    n_dev = mesh.shape[MESH_AXIS]
    row_split = P(MESH_AXIS)
    row_matrix = P(MESH_AXIS, None)
    col_matrix = P(None, MESH_AXIS)
    embed_specs = (P(None, None), P(None), P(None, None), P(None)) * 3
    in_specs = (row_split, row_split, row_matrix) + embed_specs + (col_matrix, row_split, row_matrix)
    out_specs = (row_matrix, col_matrix, row_split) + embed_specs

    def send(value, bit):
        return lax.ppermute(value, MESH_AXIS, [(i, i ^ bit) for i in range(n_dev)])

    def swap(value):
        return send(value, 1)

    def local_step(timesteps, guidance, pooled, time_w1, time_b1, time_w2, time_b2, guide_w1, guide_b1, guide_w2, guide_b2, text_w1, text_b1, text_w2, text_b2, w_mod, b_mod, d_mods):
        rows, cols = d_mods.shape[0], w_mod.shape[1]
        hidden = w_mod.shape[0]
        batch = rows * n_dev
        freq_width = time_w1.shape[0]
        params_list = [(time_w1, time_b1, time_w2, time_b2), (guide_w1, guide_b1, guide_w2, guide_b2), (text_w1, text_b1, text_w2, text_b2)]
        me = lax.axis_index(MESH_AXIS)
        core_id = lax.rem(me, 2)
        chip_id = me // 2
        core = core_id.reshape(1)

        small = jnp.concatenate([timesteps, guidance, b_mod.astype(jnp.float32)])
        small_all = lax.all_gather(small, MESH_AXIS, axis=0)
        times_all = small_all[:, :rows].reshape(-1)
        guides_all = small_all[:, rows:2 * rows].reshape(-1)
        full_bmod = small_all[:, 2 * rows:].reshape(1, -1)
        pooled_all = lax.all_gather(pooled, MESH_AXIS, axis=0, tiled=True)
        g_out = split_for_partner(core, d_mods, n_dev, cols)
        g_their = swap(g_out)

        width = cols // len(COLOURS)
        held = [{0: w_mod[:, c * width:(c + 1) * width]} for c in range(len(COLOURS))]
        for source, role in ROUNDS:
            for c, bits in enumerate(COLOURS):
                have = sum(bits[i] for i in source)
                held[c][have + bits[role]] = send(held[c][have], bits[role])

        def slices(group):
            return [lax.dynamic_slice_in_dim(d_mods, jnp.bitwise_xor(me, d) * cols, cols, axis=1) for d in group]

        g_parts = {}

        def exchange(group, after):
            parts = slices(group)
            if after is not None:
                *parts, _ = lax.optimization_barrier((*parts, after))
            for d, part in zip(group, parts):
                g_parts[d] = send(part, d)

        exchange(G_GROUPS[0], None)

        own_inputs = [sinusoid(timesteps, freq_width), sinusoid(guidance, freq_width), pooled]
        outs = [mlp_forward(inputs_bf, params) for inputs_bf, params in zip(own_inputs, params_list)]
        cond_vec = outs[0] + outs[1] + outs[2]
        cond_silu = jax.nn.silu(cond_vec).astype(jnp.bfloat16)

        all_inputs = [sinusoid(times_all, freq_width), sinusoid(guides_all, freq_width), pooled_all]
        hidden_all, part_cond = embed_half(core, all_inputs, params_list, rows)
        outgoing = lax.dynamic_slice_in_dim(part_cond, (1 - core_id) * (batch // 2), batch // 2, axis=0)
        incoming = swap(outgoing)
        bias2 = (time_b2.astype(jnp.float32) + guide_b2.astype(jnp.float32) + text_b2.astype(jnp.float32))
        mine_t = sum_silu(core, part_cond, incoming, bias2[None])
        theirs_t = swap(mine_t)

        silu_their = swap(cond_silu)
        carry = None
        n_col = len(COLOURS)
        for call in CALLS:
            pick = []
            for r in call:
                for c, bits in enumerate(COLOURS):
                    pick.append((c, 0 if r == 0 else sum(bits[j] for j in ROUNDS[r - 1][0]) + bits[ROUNDS[r - 1][1]]))
            chips = [jnp.bitwise_xor(chip_id, d // 2) for _, d in pick]
            where = jnp.stack([(2 * q + core_id) * n_col + c for q, (c, _) in zip(chips, pick)] + chips + [jnp.int32(c) for c, _ in pick])
            carry = column_rounds(where, cond_silu, silu_their, d_mods, g_their, full_bmod, [held[c][d] for c, d in pick], carry)
        modulation, mod_their, d_parts = carry
        d_other = swap(d_parts[rows:])
        d_cond = d_parts[:rows] + d_other
        d_vec = d_cond * silu_grad(cond_vec)
        d_vec_bf = d_vec.astype(jnp.bfloat16)
        sums = jnp.sum(d_vec.reshape(16, rows // 16, hidden), axis=1)
        mod_mine = swap(mod_their)
        modulation = place_blocks(core, modulation, mod_mine)
        d_vec_all = lax.all_gather(d_vec_bf, MESH_AXIS, axis=0, tiled=True)
        sums_all = lax.all_gather(sums, MESH_AXIS, axis=0, tiled=True)
        grad_b2 = jnp.sum(sums_all, axis=0)
        exchange(G_GROUPS[1], d_vec_all)
        exchange(G_GROUPS[2], d_vec_all)

        grads = {}
        for which in ((2,), (0, 1)):
            mine = embed_grad(core, d_vec_all, which, all_inputs, hidden_all, params_list, rows)
            for pos, k in enumerate(which):
                whole = []
                for value, axis in zip(mine[3 * pos:3 * pos + 3], (1, 1, 0)):
                    whole.append(join_halves(core, value, swap(value), axis))
                grads[k] = (whole[0], whole[1][0], whole[2], grad_b2)

        g_parts[1] = lax.dynamic_index_in_dim(g_their, chip_id, 0, keepdims=False)
        totals = None
        for group in ((0, 1) + G_GROUPS[0], G_GROUPS[1], G_GROUPS[2]):
            peers = [jnp.bitwise_xor(me, d) for d in group]
            where = jnp.stack([p % (n_dev // 2) for p in peers] + [(p // (n_dev // 2) == core_id).astype(jnp.int32) for p in peers] + [me])
            totals = mod_weight_grad(where, mine_t, theirs_t, [(d_mods, True) if d == 0 else (g_parts[d], False) for d in group], cols, totals)
        return (modulation, totals[0], totals[1][0]) + grads[0] + grads[1] + grads[2]


    return jax.shard_map(local_step, mesh=mesh, in_specs=in_specs, out_specs=out_specs, check_vma=False)
```

time: 1760 us -> 1430 us (0.81)
  waiting for transfers between devices: 1370 us -> 367 us
  Pallas kernels: 0 us -> 745 us
  matrix products: 259 us -> 29.8 us
  blocking collectives: 46.7 us -> 108 us
  starting transfers between devices: 0.12 us -> 45 us
  other arithmetic: 13.7 us -> 47.7 us
    reduce_scatter x1 -> x0, waiting for transfers between devices: 852 us -> none  [local_step(): lax.psum_scatter(part_wgrad, MESH_AXIS, scatter_dimension=1, tiled=True)]
    pallas_call x0 -> x23, Pallas kernels: none -> 745 us  [the longest x5 206 us: column_rounds(): pl.pallas_call(body, name='column_rounds', grid_spec=pltpu.PrefetchScalar...]
    ppermute x0 -> x50, waiting for transfers between devices: none -> 364 us  [send(): return lax.ppermute(value, MESH_AXIS, [(i, i ^ bit) for i in range(n_dev)])]
    all_gather x1 -> x3, waiting for transfers between devices: 303 us -> 2.42 us  [the longest x1 2.42 us: local_step(): sums_all = lax.all_gather(sums, MESH_AXIS, axis=0, tiled=True)]
    dot_general x15 -> x0, matrix products: 249 us -> none  [the longest x1 79.9 us: local_step(): lax.dot_general(cond_silu, d_mods, CONTRACT_ROWS, preferred_element_type=...]
    unnamed x4 -> x3, waiting for transfers between devices: 218 us -> 0.71 us
    all_gather x1, blocking collectives: 13.6 us -> 108 us  [local_step(): small_all = lax.all_gather(small, MESH_AXIS, axis=0)]
    ppermute x0 -> x50, starting transfers between devices: none -> 44.9 us  [send(): return lax.ppermute(value, MESH_AXIS, [(i, i ^ bit) for i in range(n_dev)])]
  transfers between devices with their start and end apart: 3 -> 53, of which waited for: 3 -> 17; matrix products, arithmetic and copies ran while one was open for 10% -> 9% of each run, Pallas kernels for 0% -> 51%
where the time goes in v1:
time: 1430 us; the launch traced here: 1420 us
  Pallas kernels  745 us (52%)
  waiting for transfers between devices  367 us (26%)
  blocking collectives  108 us (8%)
  local copies, waits for them, and re-layouts  58.9 us (4%)
  other arithmetic  47.7 us (3%)
  starting transfers between devices  45 us (3%)
  matrix products  29.8 us (2%)
  between operations  14.5 us (1%)
    ppermute x50, waiting for transfers between devices, send(): return lax.ppermute(value, MESH_AXIS, [(i, i ^ bit) for i in range(n_dev)])  364 us
    pallas_call x5, Pallas kernels, column_rounds(): pl.pallas_call(body, name='column_rounds', grid_spec=pltpu.PrefetchScalar...  206 us
    pallas_call x2, Pallas kernels, embed_grad(): pl.pallas_call(body, name='embed_grad', grid_spec=pltpu.PrefetchScalarGri...  182 us
    pallas_call x3, Pallas kernels, mod_weight_grad(): pl.pallas_call(body, name='mod_weight_grad', grid_spec=pltpu.PrefetchScal...  130 us
    pallas_call x1, Pallas kernels, embed_half(): pl.pallas_call(embed_body, name='embed_half', grid_spec=pltpu.PrefetchSca...  114 us
    all_gather x1, blocking collectives, local_step(): small_all = lax.all_gather(small, MESH_AXIS, axis=0)  108 us
    pallas_call x9, Pallas kernels, join_halves(): pl.pallas_call(body, name='join_halves', grid_spec=pltpu.PrefetchScalarGr...  63.9 us
    ppermute x50, starting transfers between devices, send(): return lax.ppermute(value, MESH_AXIS, [(i, i ^ bit) for i in range(n_dev)])  44.9 us
  transfers between devices with their start and end apart: 53, of which 17 were waited for; matrix products, arithmetic and copies ran while one was open for 9% of the time, Pallas kernels for 51%

profile of v1, /device:TPU:0, one launch (start us, length us, event | category | flops | bytes accessed | tf_op | source)
XLA Modules:
  0.0 1415.7 jit_solution(15481028823674456384)
XLA Ops:
  8.0 13.6 split_for_partner.1
  22.5 5.6 fusion.35
  28.1 2.5 collective-permute-start.22
  30.5 1.5 collective-permute-start.15
  32.2 2.2 fusion.12
  34.4 7.6 convolution_add_fusion.5
  42.0 8.5 fusion.5
  50.5 13.7 multiply_convert_fusion
  64.4 1.7 collective-permute-start.8
  66.1 1.6 collective-permute-done.st_ref
  67.7 1.7 collective-permute-start.20
  69.4 41.3 %collective-permute-done.22.refs_5_ = bf16[1536,640]{1,0:T(8,128)(2,1)} collective-permute-done((bf16[1536,640]{1,0:T(8,128)(2,1)}, bf16[1536,640]{1,0:T(8,128)(2,1)}, u32[]{:S(2)}, u32[]{:S(2)}) %collective-permute-start.22) | collective-permute-done | bytes 1966112 | tf_op jit(solution)/shard_map/ppermute | solution.py:371
  110.7 1.5 collective-permute-start.2
  112.8 108.4 %all-gather.1 = f32[16,1,2944]{2,1,0:T(1,128)S(1)} all-gather(f32[1,1,2944]{2,1,0:T(1,128)S(1)} %reshape.88), channel_id=2, replica_groups=mesh['fsdp'=16] {'fsdp'}, dimensions={0}, use_global_device_ids=true | all-gather | bytes 200192 | tf_op jit(solution)/shard_map/all_gather | solution.py:388
  226.6 1.5 collective-permute-start.21
  230.7 41.2 %column_rounds.5 = (bf16[512,30720]{1,0:T(8,128)(2,1)}, bf16[8,512,1920]{2,1,0:T(8,128)(2,1)}, f32[1024,1536]{1,0:T(8,128)}) custom-call(s32[18]{0:T(128)} %stack.321.where_ref, bf16[512,1536]{1,0:T(8,128)(2,1)} %copy-done.1, bf16[512,1536]{1,0:T(8,128)(2,1)} %copy-done.2, bf16[512,30720]{1,0:T(8,128)(2,1)} %refs_0_.1, ...), custom_call_target="tpu_custom_call" | custom-call | flops 24159191040 | bytes 27525120 | tf_op jit(solution)/shard_map/column_rounds/pallas_call | solution.py:134
  271.9 1.3 collective-permute-start.9
  275.1 38.8 %collective-permute-done.16.refs_2_ = bf16[1536,640]{1,0:T(8,128)(2,1)} collective-permute-done((bf16[1536,640]{1,0:T(8,128)(2,1)}, bf16[1536,640]{1,0:T(8,128)(2,1)}, u32[]{:S(2)}, u32[]{:S(2)}) %collective-permute-start.16) | collective-permute-done | bytes 1966112 | tf_op jit(solution)/shard_map/ppermute | solution.py:371
  314.7 41.3 %collective-permute-done.19.refs_5_ = bf16[1536,640]{1,0:T(8,128)(2,1)} collective-permute-done((bf16[1536,640]{1,0:T(8,128)(2,1)}, bf16[1536,640]{1,0:T(8,128)(2,1)}, u32[]{:S(2)}, u32[]{:S(2)}) %collective-permute-start.19) | collective-permute-done | bytes 1966112 | tf_op jit(solution)/shard_map/ppermute | solution.py:371
  356.8 56.5 %column_rounds.6 = (bf16[512,30720]{1,0:T(8,128)(2,1)}, bf16[8,512,1920]{2,1,0:T(8,128)(2,1)}, f32[1024,1536]{1,0:T(8,128)}) custom-call(s32[18]{0:T(128)} %stack.313.where_ref, bf16[512,1536]{1,0:T(8,128)(2,1)} %copy-done.1, bf16[512,1536]{1,0:T(8,128)(2,1)} %copy-done.2, ...), custom_call_target="tpu_custom_call", output_to_operand_aliasing={{2}: (12, {}), {0}: (13, {}), {1}: (14, {})} | custom-call | flops 24159191040 | bytes 27525120 | tf_op jit(solution)/shard_map/column_rounds/pallas_call | solution.py:134
  413.4 1.3 collective-permute-start.12
  418.8 57.0 %column_rounds.7 = (bf16[512,30720]{1,0:T(8,128)(2,1)}, bf16[8,512,1920]{2,1,0:T(8,128)(2,1)}, f32[1024,1536]{1,0:T(8,128)}) custom-call(s32[18]{0:T(128)} %stack.303.where_ref, bf16[512,1536]{1,0:T(8,128)(2,1)} %copy-done.1, bf16[512,1536]{1,0:T(8,128)(2,1)} %copy-done.2, ...), custom_call_target="tpu_custom_call", output_to_operand_aliasing={{2}: (12, {}), {0}: (13, {}), {1}: (14, {})} | custom-call | flops 24159191040 | bytes 27525120 | tf_op jit(solution)/shard_map/column_rounds/pallas_call | solution.py:134
  475.8 25.5 %column_rounds.8 = (bf16[512,30720]{1,0:T(8,128)(2,1)}, bf16[8,512,1920]{2,1,0:T(8,128)(2,1)}, f32[1024,1536]{1,0:T(8,128)}) custom-call(s32[9]{0:T(128)} %stack.296.where_ref, bf16[512,1536]{1,0:T(8,128)(2,1)} %copy-done.1, bf16[512,1536]{1,0:T(8,128)(2,1)} %copy-done.2, ...), custom_call_target="tpu_custom_call", output_to_operand_aliasing={{2}: (9, {}), {0}: (10, {}), {1}: (11, {})} | custom-call | flops 12079595520 | bytes 13762560 | tf_op jit(solution)/shard_map/column_rounds/pallas_call | solution.py:134
  503.3 25.9 %column_rounds.9 = (bf16[512,30720]{1,0:T(8,128)(2,1)}, bf16[8,512,1920]{2,1,0:T(8,128)(2,1)}, f32[1024,1536]{1,0:T(8,128)}) custom-call(s32[9]{0:T(128)} %stack.289.where_ref, bf16[512,1536]{1,0:T(8,128)(2,1)} %copy-done.1, bf16[512,1536]{1,0:T(8,128)(2,1)} %copy-done.2, ...), custom_call_target="tpu_custom_call", output_to_operand_aliasing={{2}: (9, {}), {0}: (10, {}), {1}: (11, {})} | custom-call | flops 12079595520 | bytes 13762560 | tf_op jit(solution)/shard_map/column_rounds/pallas_call | solution.py:134
  529.1 2.2 slice.31
  531.4 5.6 collective-permute-done.26
  537.1 3.5 bitcast_reduce_fusion
  543.3 30.5 %fusion.2 = (bf16[8192,128]{1,0:T(8,128)(2,1)S(1)}, bf16[8192,128]{1,0:T(8,128)(2,1)S(1)}, bf16[8192,128]{1,0:T(8,128)(2,1)S(1)}, bf16[8192,128]{1,0:T(8,128)(2,1)S(1)}) fusion(f32[8192]{0:T(1024)S(1)} %bitcast.97, f32[128]{0:T(128)S(1)} %copy-done.32, f32[8192]{0:T(1024)S(1)} %bitcast.98), kind=kLoop, calls=%fused_computation.6 | loop fusion | flops 6291456 | bytes 8454656 | tf_op jit(solution)/shard_map/convert.16
  573.9 3.9 pad_maximum_fusion
  577.7 114.4 %embed_half.1 = (f32[3,8192,768]{2,1,0:T(8,128)}, f32[8192,1536]{1,0:T(8,128)}) custom-call(s32[1]{0:T(128)} %bitcast.core_ref, bf16[8192,256]{1,0:T(8,128)(2,1)} %get-tuple-element.132.t_ref.refs_1_, bf16[8192,256]{1,0:T(8,128)(2,1)} %get-tuple-element.133.g_ref.refs_2_, bf16[8192,2048]{1,0:T(8,128)(2,1)} %all-gather.6.cloned.1.call-done.u_ref.refs_1_, ...), custom_call_target="tpu_custom_call" | custom-call | flops 90194313216 | bytes 125829120 | tf_op jit(solution)/shard_map/embed_half/pallas_call | solution.py:194
  692.1 17.4 %constant_dynamic-slice_fusion.14 = f32[4096,1536]{1,0:T(8,128)} fusion(f32[8192,1536]{1,0:T(8,128)} %get-tuple-element.69.a_ref, s32[]{:T(128)S(6)} %select_n.173), kind=kLoop, calls=%fused_computation.66 | loop fusion | bytes 50331652 | tf_op jit(solution)/shard_map/dynamic_slice | solution.py:424
  710.0 18.0 %constant_dynamic-slice_fusion = (bf16[512,1920]{1,0:T(8,128)(2,1)}, bf16[512,1920]{1,0:T(8,128)(2,1)}, bf16[512,1920]{1,0:T(8,128)(2,1)}, bf16[512,1920]{1,0:T(...) fusion(bf16[512,30720]{1,0:T(8,128)(2,1)} %refs_0_.1, ...), kind=kLoop, calls=%fused_computation.52 | loop fusion | bytes 55050296 | tf_op jit(solution)/shard_map/dynamic_slice | solution.py:404
  728.1 1.3 collective-permute-start.40
  731.6 81.1 %embed_grad.3 = (f32[2048,768]{1,0:T(8,128)}, f32[1,768]{1,0:T(1,128)}, f32[768,1536]{1,0:T(8,128)}) custom-call(s32[1]{0:T(128)} %bitcast.core_ref, bf16[8192,1536]{1,0:T(8,128)(2,1)} %all-gather.8.cloned.1.call-done.refs_0_, bf16[8192,2048]{1,0:T(8,128)(2,1)} %all-gather.6.cloned.1.call-done.u_ref.refs_1_, ...), custom_call_target="tpu_custom_call" | custom-call | flops 64424509440 | bytes 75497472 | tf_op jit(solution)/shard_map/embed_grad/pallas_call | solution.py:244
  813.4 21.1 %sum_silu.1.mine_ref = bf16[1536,4096]{1,0:T(8,128)(2,1)} custom-call(s32[1]{0:T(128)} %bitcast.core_ref, f32[8192,1536]{1,0:T(8,128)} %get-tuple-element.69.a_ref, f32[4096,1536]{1,0:T(8,128)} %collective-permute-done.24.b_ref, f32[1,1536]{1,0:T(1,128)} %broadcast_in_dim.11.bias_ref), custom_call_target="tpu_custom_call" | custom-call | flops 50331648 | bytes 62914560 | tf_op jit(solution)/shard_map/sum_silu/pallas_call | solution.py:159
  836.2 101.1 %embed_grad.2 = (f32[256,768]{1,0:T(8,128)}, f32[1,768]{1,0:T(1,128)}, f32[768,1536]{1,0:T(8,128)}, f32[256,768]{1,0:T(8,128)}, f32[1,768]{1,0:T(1,128)}, /*index=5*/f32[768,1536]{1,0:T(8,128)}) custom-call(s32[1]{0:T(128)} %bitcast.core_ref, bf16[8192,1536]{1,0:T(8,128)(2,1)} %all-gather.8.cloned.1.call-done.refs_0_, ...), custom_call_target="tpu_custom_call" | custom-call | flops 83751862272 | bytes 75497472 | tf_op jit(solution)/shard_map/embed_grad/pallas_call | solution.py:244
  938.2 2.7 collective-permute-done.48.theirs_ref
  944.6 7.4 collective-permute-done.49.theirs_ref
  952.5 6.2 collective-permute-done.43.theirs_ref
  958.7 1.3 collective-permute-start.29
  960.1 5.4 collective-permute-done.46.theirs_ref
  969.8 3.1 dynamic-slice_bitcast_fusion.refs_1_
  972.9 2.4 all-gather.10.cloned.1.call-done
  975.3 1.5 reduce_sum.19
  976.9 13.2 place_blocks.1
  994.0 1.3 reduce.3
  995.3 1.3 reduce.1
  997.9 5.8 join_halves.9
  1003.7 5.8 join_halves.12
  1009.6 11.5 join_halves.17
  1021.1 11.5 join_halves.11
  1032.5 11.5 join_halves.14
  1044.0 14.0 join_halves.15
  1058.0 2.4 collective-permute-start.27
  1061.4 23.7 %collective-permute-done.30.refs_1_ = bf16[512,1920]{1,0:T(8,128)(2,1)} collective-permute-done((bf16[512,1920]{1,0:T(8,128)(2,1)}, bf16[512,1920]{1,0:T(8,128)(2,1)}, u32[]{:S(2)}, u32[]{:S(2)}) %collective-permute-start.30) | collective-permute-done | bytes 1966112 | tf_op jit(solution)/shard_map/ppermute | solution.py:371
  1085.1 2.6 collective-permute-start.32
  1087.7 41.2 %collective-permute-done.31.refs_2_ = bf16[512,1920]{1,0:T(8,128)(2,1)} collective-permute-done((bf16[512,1920]{1,0:T(8,128)(2,1)}, bf16[512,1920]{1,0:T(8,128)(2,1)}, u32[]{:S(2)}, u32[]{:S(2)}) %collective-permute-start.31) | collective-permute-done | bytes 1966112 | tf_op jit(solution)/shard_map/ppermute | solution.py:371
  1130.0 62.7 %mod_weight_grad.3 = (f32[1536,1920]{1,0:T(8,128)}, f32[1,1920]{1,0:T(1,128)}) custom-call(s32[17]{0:T(128)} %stack.373.where_ref, bf16[1536,4096]{1,0:T(8,128)(2,1)} %sum_silu.1.mine_ref, bf16[1536,4096]{1,0:T(8,128)(2,1)} %collective-permute-done.25.theirs_ref, bf16[512,30720]{1,0:T(8,128)(2,1)} %refs_0_.1, ...), custom_call_target="tpu_custom_call" | custom-call | flops 24159191040 | bytes 77070336 | tf_op jit(solution)/shard_map/mod_weight_grad/pallas_call | solution.py:310
  1192.7 102.7 %collective-permute-done.32.refs_3_ = bf16[512,1920]{1,0:T(8,128)(2,1)} collective-permute-done((bf16[512,1920]{1,0:T(8,128)(2,1)}, bf16[512,1920]{1,0:T(8,128)(2,1)}, u32[]{:S(2)}, u32[]{:S(2)}) %collective-permute-start.32) | collective-permute-done | bytes 1966112 | tf_op jit(solution)/shard_map/ppermute | solution.py:371
  1295.4 1.7 collective-permute-done.33.refs_4_
  1297.1 41.9 %collective-permute-done.34.refs_5_ = bf16[512,1920]{1,0:T(8,128)(2,1)} collective-permute-done((bf16[512,1920]{1,0:T(8,128)(2,1)}, bf16[512,1920]{1,0:T(8,128)(2,1)}, u32[]{:S(2)}, u32[]{:S(2)}) %collective-permute-start.34) | collective-permute-done | bytes 1966112 | tf_op jit(solution)/shard_map/ppermute | solution.py:371
  1339.0 46.1 %mod_weight_grad.4 = (f32[1536,1920]{1,0:T(8,128)}, f32[1,1920]{1,0:T(1,128)}) custom-call(s32[13]{0:T(128)} %stack.348.where_ref, bf16[1536,4096]{1,0:T(8,128)(2,1)} %sum_silu.1.mine_ref, bf16[1536,4096]{1,0:T(8,128)(2,1)} %collective-permute-done.25.theirs_ref, ...), custom_call_target="tpu_custom_call", output_to_operand_aliasing={{0}: (9, {}), {1}: (10, {})} | custom-call | flops 18119393280 | bytes 63700992 | tf_op jit(solution)/shard_map/mod_weight_grad/pallas_call | solution.py:310
  1385.2 21.3 %mod_weight_grad.5 = (f32[1536,1920]{1,0:T(8,128)}, f32[1,1920]{1,0:T(1,128)}) custom-call(s32[5]{0:T(128)} %stack.329.where_ref, bf16[1536,4096]{1,0:T(8,128)(2,1)} %sum_silu.1.mine_ref, bf16[1536,4096]{1,0:T(8,128)(2,1)} %collective-permute-done.25.theirs_ref, ...), custom_call_target="tpu_custom_call", output_to_operand_aliasing={{0}: (5, {}), {1}: (6, {})} | custom-call | flops 6039797760 | bytes 36962304 | tf_op jit(solution)/shard_map/mod_weight_grad/pallas_call | solution.py:310
  1406.5 1.3 reduce
  (188 shorter events, 45.7 us)
Async XLA Ops:
  7.2 570.5 %all-gather.6.cloned.1.call-start = ((), (), s32[]{:S(2)}) async-start(), calls=%async_computation | async-start | bytes 35651584 | tf_op jit(solution)/shard_map/all_gather | solution.py:392
  7.9 723.6 %all-gather.8.cloned.1.call-start = ((), (), s32[]{:S(2)}) async-start(), calls=%async_computation.1 | async-start | bytes 26738688 | tf_op jit(solution)/shard_map/all_gather | solution.py:449
  21.7 208.3 %collective-permute-start.1 = (bf16[8,512,1920]{2,1,0:T(8,128)(2,1)}, bf16[8,512,1920]{2,1,0:T(8,128)(2,1)}, u32[]{:S(2)}, u32[]{:S(2)}) collective-permute-start(bf16[8,512,1920]{2,1,0:T(8,128)(2,1)} %split_for_partner.1), channel_id=1, source_target_pairs={{0,1},{1,0},{2,3},{3,2},{4,5},{5,4},{6,7},{7,6},{8,9},{9,8},{10,11... | collective-permute-start | bytes 47185928 | tf_op jit(solution)/shard_map/ppermute | solution.py:371
  28.1 82.7 %collective-permute-start.22 = (bf16[1536,640]{1,0:T(8,128)(2,1)}, bf16[1536,640]{1,0:T(8,128)(2,1)}, u32[]{:S(2)}, u32[]{:S(2)}) collective-permute-start(bf16[1536,640]{1,0:T(8,128)(2,1)} %get-tuple-element.111.refs_2_), channel_id=1, source_target_pairs={{0,4},{1,5},{2,6},{3,7},{4,0},{5,1},{6,2},{7,3},{8,12},{9,13},{10,... | collective-permute-start | bytes 5898248 | tf_op jit(solution)/shard_map/ppermute | solution.py:371
  30.5 81.7 %collective-permute-start.15 = (bf16[1536,640]{1,0:T(8,128)(2,1)}, bf16[1536,640]{1,0:T(8,128)(2,1)}, u32[]{:S(2)}, u32[]{:S(2)}) collective-permute-start(bf16[1536,640]{1,0:T(8,128)(2,1)} %get-tuple-element.111.refs_2_), channel_id=1, source_target_pairs={{0,2},{1,3},{2,0},{3,1},{4,6},{5,7},{6,4},{7,5},{8,10},{9,11},{10,... | collective-permute-start | bytes 5898248 | tf_op jit(solution)/shard_map/ppermute | solution.py:371
  50.5 62.2 %copy-start.26 = (bf16[1920]{0:T(1024)(128)(2,1)S(1)}, bf16[1920]{0:T(1024)(128)(2,1)}, u32[]{:S(2)}) copy-start(bf16[1920]{0:T(1024)(128)(2,1)} %param.34) | copy-start | bytes 11524
  64.3 166.4 %copy-start.1 = (bf16[512,1536]{1,0:T(8,128)(2,1)}, bf16[512,1536]{1,0:T(8,128)(2,1)S(1)}, u32[]{:S(2)}) copy-start(bf16[512,1536]{1,0:T(8,128)(2,1)S(1)} %get-tuple-element.128.so_ref) | copy-start | bytes 4718596
  64.3 3.4 collective-permute-start
  64.4 161.3 %collective-permute-start.8 = (bf16[1536,640]{1,0:T(8,128)(2,1)}, bf16[1536,640]{1,0:T(8,128)(2,1)}, u32[]{:S(2)}, u32[]{:S(2)}) collective-permute-start(bf16[1536,640]{1,0:T(8,128)(2,1)} %get-tuple-element.111.refs_2_), channel_id=1, source_target_pairs={{0,8},{1,9},{2,10},{3,11},{4,12},{5,13},{6,14},{7,15},{8,0},{9,1},... | collective-permute-start | bytes 5898248 | tf_op jit(solution)/shard_map/ppermute | solution.py:371
  67.7 163.0 %copy-start.2 = (bf16[512,1536]{1,0:T(8,128)(2,1)}, bf16[512,1536]{1,0:T(8,128)(2,1)S(1)}, u32[]{:S(2)}) copy-start(bf16[512,1536]{1,0:T(8,128)(2,1)S(1)} %collective-permute-done.st_ref) | copy-start | bytes 4718596
  67.7 158.9 %collective-permute-start.20 = (bf16[1536,640]{1,0:T(8,128)(2,1)}, bf16[1536,640]{1,0:T(8,128)(2,1)}, u32[]{:S(2)}, u32[]{:S(2)}) collective-permute-start(bf16[1536,640]{1,0:T(8,128)(2,1)} %get-tuple-element.112.refs_0_), channel_id=1, source_target_pairs={{0,8},{1,9},{2,10},{3,11},{4,12},{5,13},{6,14},{7,15},{8,0},{9,1},... | collective-permute-start | bytes 5898248 | tf_op jit(solution)/shard_map/ppermute | solution.py:371
  110.7 117.4 %collective-permute-start.2 = (bf16[1536,640]{1,0:T(8,128)(2,1)}, bf16[1536,640]{1,0:T(8,128)(2,1)}, u32[]{:S(2)}, u32[]{:S(2)}) collective-permute-start(bf16[1536,640]{1,0:T(8,128)(2,1)} %get-tuple-element.112.refs_0_), channel_id=1, source_target_pairs={{0,2},{1,3},{2,0},{3,1},{4,6},{5,7},{6,4},{7,5},{8,10},{9,11},{10,... | collective-permute-start | bytes 5898248 | tf_op jit(solution)/shard_map/ppermute | solution.py:371
  112.2 116.5 %collective-permute-start.5 = (bf16[1536,640]{1,0:T(8,128)(2,1)}, bf16[1536,640]{1,0:T(8,128)(2,1)}, u32[]{:S(2)}, u32[]{:S(2)}) collective-permute-start(bf16[1536,640]{1,0:T(8,128)(2,1)} %get-tuple-element.113.refs_1_), channel_id=1, source_target_pairs={{0,4},{1,5},{2,6},{3,7},{4,0},{5,1},{6,2},{7,3},{8,12},{9,13},{10,... | collective-permute-start | bytes 5898248 | tf_op jit(solution)/shard_map/ppermute | solution.py:371
  225.8 46.2 %collective-permute-start.11 = (bf16[1536,640]{1,0:T(8,128)(2,1)}, bf16[1536,640]{1,0:T(8,128)(2,1)}, u32[]{:S(2)}, u32[]{:S(2)}) collective-permute-start(bf16[1536,640]{1,0:T(8,128)(2,1)} %get-tuple-element.112.refs_0_), channel_id=1, source_target_pairs={{0,4},{1,5},{2,6},{3,7},{4,0},{5,1},{6,2},{7,3},{8,12},{9,13},{10,... | collective-permute-start | bytes 5898248 | tf_op jit(solution)/shard_map/ppermute | solution.py:371
  226.6 46.7 %collective-permute-start.21 = (bf16[1536,640]{1,0:T(8,128)(2,1)}, bf16[1536,640]{1,0:T(8,128)(2,1)}, u32[]{:S(2)}, u32[]{:S(2)}) collective-permute-start(bf16[1536,640]{1,0:T(8,128)(2,1)} %get-tuple-element.113.refs_1_), channel_id=1, source_target_pairs={{0,2},{1,3},{2,0},{3,1},{4,6},{5,7},{6,4},{7,5},{8,10},{9,11},{10,... | collective-permute-start | bytes 5898248 | tf_op jit(solution)/shard_map/ppermute | solution.py:371
  228.1 45.8 %collective-permute-start.13 = (bf16[1536,640]{1,0:T(8,128)(2,1)}, bf16[1536,640]{1,0:T(8,128)(2,1)}, u32[]{:S(2)}, u32[]{:S(2)}) collective-permute-start(bf16[1536,640]{1,0:T(8,128)(2,1)} %get-tuple-element.113.refs_1_), channel_id=1, source_target_pairs={{0,8},{1,9},{2,10},{3,11},{4,12},{5,13},{6,14},{7,15},{8,0},{9,1},... | collective-permute-start | bytes 5898248 | tf_op jit(solution)/shard_map/ppermute | solution.py:371
  228.7 85.2 %collective-permute-start.16 = (bf16[1536,640]{1,0:T(8,128)(2,1)}, bf16[1536,640]{1,0:T(8,128)(2,1)}, u32[]{:S(2)}, u32[]{:S(2)}) collective-permute-start(bf16[1536,640]{1,0:T(8,128)(2,1)} %collective-permute-done.15.refs_2_), channel_id=1, source_target_pairs={{0,4},{1,5},{2,6},{3,7},{4,0},{5,1},{6,2},{7,3},{8,12},{9,13},{10,... | collective-permute-start | bytes 5898248 | tf_op jit(solution)/shard_map/ppermute | solution.py:371
  230.0 126.1 %collective-permute-start.19 = (bf16[1536,640]{1,0:T(8,128)(2,1)}, bf16[1536,640]{1,0:T(8,128)(2,1)}, u32[]{:S(2)}, u32[]{:S(2)}) collective-permute-start(bf16[1536,640]{1,0:T(8,128)(2,1)} %collective-permute-done.8.refs_5_), channel_id=1, source_target_pairs={{0,4},{1,5},{2,6},{3,7},{4,0},{5,1},{6,2},{7,3},{8,12},{9,13},{10,... | collective-permute-start | bytes 5898248 | tf_op jit(solution)/shard_map/ppermute | solution.py:371
  271.9 141.4 %collective-permute-start.9 = (bf16[1536,640]{1,0:T(8,128)(2,1)}, bf16[1536,640]{1,0:T(8,128)(2,1)}, u32[]{:S(2)}, u32[]{:S(2)}) collective-permute-start(bf16[1536,640]{1,0:T(8,128)(2,1)} %collective-permute-done.8.refs_5_), channel_id=1, source_target_pairs={{0,2},{1,3},{2,0},{3,1},{4,6},{5,7},{6,4},{7,5},{8,10},{9,11},{10,... | collective-permute-start | bytes 5898248 | tf_op jit(solution)/shard_map/ppermute | solution.py:371
  273.3 141.4 %collective-permute-start.17 = (bf16[1536,640]{1,0:T(8,128)(2,1)}, bf16[1536,640]{1,0:T(8,128)(2,1)S(1)}, u32[]{:S(2)}, u32[]{:S(2)}) collective-permute-start(bf16[1536,640]{1,0:T(8,128)(2,1)} %collective-permute-done.2.refs_3_), channel_id=1, source_target_pairs={{0,8},{1,9},{2,10},{3,11},{4,12},{5,13},{6,14},{7,15},{8,0},{9,1},... | collective-permute-start | bytes 5898248 | tf_op jit(solution)/shard_map/ppermute | solution.py:371
  273.9 142.0 %collective-permute-start.3 = (bf16[1536,640]{1,0:T(8,128)(2,1)}, bf16[1536,640]{1,0:T(8,128)(2,1)}, u32[]{:S(2)}, u32[]{:S(2)}) collective-permute-start(bf16[1536,640]{1,0:T(8,128)(2,1)} %collective-permute-done.2.refs_3_), channel_id=1, source_target_pairs={{0,4},{1,5},{2,6},{3,7},{4,0},{5,1},{6,2},{7,3},{8,12},{9,13},{10,... | collective-permute-start | bytes 5898248 | tf_op jit(solution)/shard_map/ppermute | solution.py:371
  313.9 103.1 %collective-permute-start.18 = (bf16[1536,640]{1,0:T(8,128)(2,1)}, bf16[1536,640]{1,0:T(8,128)(2,1)}, u32[]{:S(2)}, u32[]{:S(2)}) collective-permute-start(bf16[1536,640]{1,0:T(8,128)(2,1)} %collective-permute-done.5.refs_4_), channel_id=1, source_target_pairs={{0,2},{1,3},{2,0},{3,1},{4,6},{5,7},{6,4},{7,5},{8,10},{9,11},{10,... | collective-permute-start | bytes 5898248 | tf_op jit(solution)/shard_map/ppermute | solution.py:371
  356.0 62.1 %collective-permute-start.6 = (bf16[1536,640]{1,0:T(8,128)(2,1)}, bf16[1536,640]{1,0:T(8,128)(2,1)}, u32[]{:S(2)}, u32[]{:S(2)}) collective-permute-start(bf16[1536,640]{1,0:T(8,128)(2,1)} %collective-permute-done.5.refs_4_), channel_id=1, source_target_pairs={{0,8},{1,9},{2,10},{3,11},{4,12},{5,13},{6,14},{7,15},{8,0},{9,1},... | collective-permute-start | bytes 5898248 | tf_op jit(solution)/shard_map/ppermute | solution.py:371
  413.4 62.4 %collective-permute-start.12 = (bf16[1536,640]{1,0:T(8,128)(2,1)}, bf16[1536,640]{1,0:T(8,128)(2,1)}, u32[]{:S(2)}, u32[]{:S(2)}) collective-permute-start(bf16[1536,640]{1,0:T(8,128)(2,1)} %collective-permute-done.11.refs_0_), channel_id=1, source_target_pairs={{0,8},{1,9},{2,10},{3,11},{4,12},{5,13},{6,14},{7,15},{8,0},{9,1},... | collective-permute-start | bytes 5898248 | tf_op jit(solution)/shard_map/ppermute | solution.py:371
  414.7 61.1 %collective-permute-start.14 = (bf16[1536,640]{1,0:T(8,128)(2,1)}, bf16[1536,640]{1,0:T(8,128)(2,1)}, u32[]{:S(2)}, u32[]{:S(2)}) collective-permute-start(bf16[1536,640]{1,0:T(8,128)(2,1)} %collective-permute-done.13.refs_1_), channel_id=1, source_target_pairs={{0,2},{1,3},{2,0},{3,1},{4,6},{5,7},{6,4},{7,5},{8,10},{9,11},{10,... | collective-permute-start | bytes 5898248 | tf_op jit(solution)/shard_map/ppermute | solution.py:371
  416.0 85.4 %collective-permute-start.10 = (bf16[1536,640]{1,0:T(8,128)(2,1)}, bf16[1536,640]{1,0:T(8,128)(2,1)S(1)}, u32[]{:S(2)}, u32[]{:S(2)}) collective-permute-start(bf16[1536,640]{1,0:T(8,128)(2,1)} %collective-permute-done.9.refs_2_), channel_id=1, source_target_pairs={{0,4},{1,5},{2,6},{3,7},{4,0},{5,1},{6,2},{7,3},{8,12},{9,13},{10,... | collective-permute-start | bytes 5898248 | tf_op jit(solution)/shard_map/ppermute | solution.py:371
  417.0 84.4 %collective-permute-start.4 = (bf16[1536,640]{1,0:T(8,128)(2,1)}, bf16[1536,640]{1,0:T(8,128)(2,1)S(1)}, u32[]{:S(2)}, u32[]{:S(2)}) collective-permute-start(bf16[1536,640]{1,0:T(8,128)(2,1)} %collective-permute-done.3.refs_0_), channel_id=1, source_target_pairs={{0,8},{1,9},{2,10},{3,11},{4,12},{5,13},{6,14},{7,15},{8,0},{9,1},... | collective-permute-start | bytes 5898248 | tf_op jit(solution)/shard_map/ppermute | solution.py:371
  418.1 83.3 %collective-permute-start.7 = (bf16[1536,640]{1,0:T(8,128)(2,1)}, bf16[1536,640]{1,0:T(8,128)(2,1)}, u32[]{:S(2)}, u32[]{:S(2)}) collective-permute-start(bf16[1536,640]{1,0:T(8,128)(2,1)} %collective-permute-done.6.refs_1_), channel_id=1, source_target_pairs={{0,2},{1,3},{2,0},{3,1},{4,6},{5,7},{6,4},{7,5},{8,10},{9,11},{10,... | collective-permute-start | bytes 5898248 | tf_op jit(solution)/shard_map/ppermute | solution.py:371
  503.3 33.8 %copy-start.3 = (f32[512,1536]{1,0:T(8,128)S(1)}, f32[512,1536]{1,0:T(8,128)}, u32[]{:S(2)}) copy-start(f32[512,1536]{1,0:T(8,128)} %get-tuple-element.129) | copy-start | bytes 9437188
  531.4 5.7 collective-permute-start.26
  540.7 434.7 %all-gather.10.cloned.1.call-start = ((), (), s32[]{:S(2)}) async-start(), calls=%async_computation.2 | async-start | bytes 1671168 | tf_op jit(solution)/shard_map/all_gather | solution.py:450
  709.5 103.1 %collective-permute-start.24 = (f32[4096,1536]{1,0:T(8,128)}, f32[4096,1536]{1,0:T(8,128)}, u32[]{:S(2)}, u32[]{:S(2)}) collective-permute-start(f32[4096,1536]{1,0:T(8,128)} %constant_dynamic-slice_fusion.14), channel_id=1, source_target_pairs={{0,1},{1,0},{2,3},{3,2},{4,5},{5,4},{6,7},{7,6},{8,9},{9,8},{10,11... | collective-permute-start | bytes 75497480 | tf_op jit(solution)/shard_map/ppermute | solution.py:371
  709.7 228.2 %collective-permute-start.23 = (bf16[8,512,1920]{2,1,0:T(8,128)(2,1)}, bf16[8,512,1920]{2,1,0:T(8,128)(2,1)}, u32[]{:S(2)}, u32[]{:S(2)}) collective-permute-start(bf16[8,512,1920]{2,1,0:T(8,128)(2,1)} %get-tuple-element.67), channel_id=1, source_target_pairs={{0,1},{1,0},{2,3},{3,2},{4,5},{5,4},{6,7},{7,6},{8,9},{9,8},{10,11... | collective-permute-start | bytes 47185928 | tf_op jit(solution)/shard_map/ppermute | solution.py:371
  728.1 106.4 %collective-permute-start.40 = (bf16[512,1920]{1,0:T(8,128)(2,1)}, bf16[512,1920]{1,0:T(8,128)(2,1)}, u32[]{:S(2)}, u32[]{:S(2)}) collective-permute-start(bf16[512,1920]{1,0:T(8,128)(2,1)} %get-tuple-element.97), channel_id=1, source_target_pairs={{0,9},{1,8},{2,11},{3,10},{4,13},{5,12},{6,15},{7,14},{8,1},{9,0},... | collective-permute-start | bytes 5898248 | tf_op jit(solution)/shard_map/ppermute | solution.py:371
  729.4 106.3 %collective-permute-start.39 = (bf16[512,1920]{1,0:T(8,128)(2,1)}, bf16[512,1920]{1,0:T(8,128)(2,1)}, u32[]{:S(2)}, u32[]{:S(2)}) collective-permute-start(bf16[512,1920]{1,0:T(8,128)(2,1)} %get-tuple-element.98), channel_id=1, source_target_pairs={{0,8},{1,9},{2,10},{3,11},{4,12},{5,13},{6,14},{7,15},{8,0},{9,1},... | collective-permute-start | bytes 5898248 | tf_op jit(solution)/shard_map/ppermute | solution.py:371
  729.9 106.2 %collective-permute-start.38 = (bf16[512,1920]{1,0:T(8,128)(2,1)}, bf16[512,1920]{1,0:T(8,128)(2,1)}, u32[]{:S(2)}, u32[]{:S(2)}) collective-permute-start(bf16[512,1920]{1,0:T(8,128)(2,1)} %get-tuple-element.99), channel_id=1, source_target_pairs={{0,5},{1,4},{2,7},{3,6},{4,1},{5,0},{6,3},{7,2},{8,13},{9,12},{10,... | collective-permute-start | bytes 5898248 | tf_op jit(solution)/shard_map/ppermute | solution.py:371
  812.7 124.6 %collective-permute-start.37 = (bf16[512,1920]{1,0:T(8,128)(2,1)}, bf16[512,1920]{1,0:T(8,128)(2,1)}, u32[]{:S(2)}, u32[]{:S(2)}) collective-permute-start(bf16[512,1920]{1,0:T(8,128)(2,1)} %get-tuple-element.100), channel_id=1, source_target_pairs={{0,4},{1,5},{2,6},{3,7},{4,0},{5,1},{6,2},{7,3},{8,12},{9,13},{10,... | collective-permute-start | bytes 5898248 | tf_op jit(solution)/shard_map/ppermute | solution.py:371
  834.4 103.2 %collective-permute-start.36 = (bf16[512,1920]{1,0:T(8,128)(2,1)S(1)}, bf16[512,1920]{1,0:T(8,128)(2,1)}, u32[]{:S(2)}, u32[]{:S(2)}) collective-permute-start(bf16[512,1920]{1,0:T(8,128)(2,1)S(1)} %get-tuple-element.101), channel_id=1, source_target_pairs={{0,3},{1,2},{2,1},{3,0},{4,7},{5,6},{6,5},{7,4},{8,11},{9,10},{10,... | collective-permute-start | bytes 5898248 | tf_op jit(solution)/shard_map/ppermute | solution.py:371
  835.7 102.1 %copy-start.27 = (f32[1,768]{1,0:T(1,128)S(1)}, f32[1,768]{1,0:T(1,128)}, u32[]{:S(2)}) copy-start(f32[1,768]{1,0:T(1,128)} %get-tuple-element.93.mine_ref) | copy-start | bytes 9220
  835.7 131.1 %collective-permute-start.47 = (f32[2048,768]{1,0:T(8,128)}, f32[2048,768]{1,0:T(8,128)}, u32[]{:S(2)}, u32[]{:S(2)}) collective-permute-start(f32[2048,768]{1,0:T(8,128)} %get-tuple-element.92.mine_ref), channel_id=1, source_target_pairs={{0,1},{1,0},{2,3},{3,2},{4,5},{5,4},{6,7},{7,6},{8,9},{9,8},{10,11... | collective-permute-start | bytes 18874376 | tf_op jit(solution)/shard_map/ppermute | solution.py:371
  836.1 293.9 %collective-permute-start.25 = (bf16[1536,4096]{1,0:T(8,128)(2,1)}, bf16[1536,4096]{1,0:T(8,128)(2,1)}, u32[]{:S(2)}, u32[]{:S(2)}) collective-permute-start(bf16[1536,4096]{1,0:T(8,128)(2,1)} %sum_silu.1.mine_ref), channel_id=1, source_target_pairs={{0,1},{1,0},{2,3},{3,2},{4,5},{5,4},{6,7},{7,6},{8,9},{9,8},{10,11... | collective-permute-start | bytes 37748744 | tf_op jit(solution)/shard_map/ppermute | solution.py:371
  937.3 6.8 collective-permute-start.41
  937.7 6.6 collective-permute-start.44
  937.8 3.1 collective-permute-start.48
  940.9 35.9 %copy-start.28 = (f32[1,768]{1,0:T(1,128)}, f32[1,768]{1,0:T(1,128)S(1)}, u32[]{:S(2)}) copy-start(f32[1,768]{1,0:T(1,128)S(1)} %collective-permute-done.48.theirs_ref) | copy-start | bytes 9220
  940.9 1.4 collective-permute-start.42
  942.3 34.5 %copy-start.29 = (f32[1,768]{1,0:T(1,128)}, f32[1,768]{1,0:T(1,128)S(1)}, u32[]{:S(2)}) copy-start(f32[1,768]{1,0:T(1,128)S(1)} %collective-permute-done.42.theirs_ref) | copy-start | bytes 9220
  942.3 1.4 collective-permute-start.45
  943.7 33.1 %copy-start.30 = (f32[1,768]{1,0:T(1,128)}, f32[1,768]{1,0:T(1,128)S(1)}, u32[]{:S(2)}) copy-start(f32[1,768]{1,0:T(1,128)S(1)} %collective-permute-done.45.theirs_ref) | copy-start | bytes 9220
  943.7 8.3 collective-permute-start.49
  944.1 32.8 %copy-start.8 = (f32[256,768]{1,0:T(8,128)}, f32[256,768]{1,0:T(8,128)S(1)}, u32[]{:S(2)}) copy-start(f32[256,768]{1,0:T(8,128)S(1)} %collective-permute-done.41.theirs_ref) | copy-start | bytes 2359300
  944.1 14.7 %collective-permute-start.43 = (f32[768,1536]{1,0:T(8,128)}, f32[768,1536]{1,0:T(8,128)}, u32[]{:S(2)}, u32[]{:S(2)}) collective-permute-start(f32[768,1536]{1,0:T(8,128)} %get-tuple-element.88.mine_ref), channel_id=1, source_target_pairs={{0,1},{1,0},{2,3},{3,2},{4,5},{5,4},{6,7},{7,6},{8,9},{9,8},{10,11... | collective-permute-start | bytes 14155784 | tf_op jit(solution)/shard_map/ppermute | solution.py:371
  944.2 32.6 %copy-start.9 = (f32[256,768]{1,0:T(8,128)}, f32[256,768]{1,0:T(8,128)S(1)}, u32[]{:S(2)}) copy-start(f32[256,768]{1,0:T(8,128)S(1)} %collective-permute-done.44.theirs_ref) | copy-start | bytes 2359300
  944.2 21.2 %collective-permute-start.46 = (f32[768,1536]{1,0:T(8,128)}, f32[768,1536]{1,0:T(8,128)}, u32[]{:S(2)}, u32[]{:S(2)}) collective-permute-start(f32[768,1536]{1,0:T(8,128)} %get-tuple-element.91.mine_ref), channel_id=1, source_target_pairs={{0,1},{1,0},{2,3},{3,2},{4,5},{5,4},{6,7},{7,6},{8,9},{9,8},{10,11... | collective-permute-start | bytes 14155784 | tf_op jit(solution)/shard_map/ppermute | solution.py:371
  952.0 106.0 %collective-permute-start.35 = (bf16[512,1920]{1,0:T(8,128)(2,1)}, bf16[512,1920]{1,0:T(8,128)(2,1)}, u32[]{:S(2)}, u32[]{:S(2)}) collective-permute-start(bf16[512,1920]{1,0:T(8,128)(2,1)} %get-tuple-element.102), channel_id=1, source_target_pairs={{0,2},{1,3},{2,0},{3,1},{4,6},{5,7},{6,4},{7,5},{8,10},{9,11},{10,... | collective-permute-start | bytes 5898248 | tf_op jit(solution)/shard_map/ppermute | solution.py:371
  958.7 101.6 %collective-permute-start.29 = (bf16[512,1920]{1,0:T(8,128)(2,1)}, bf16[512,1920]{1,0:T(8,128)(2,1)}, u32[]{:S(2)}, u32[]{:S(2)}) collective-permute-start(bf16[512,1920]{1,0:T(8,128)(2,1)} %get-tuple-element.73), channel_id=1, source_target_pairs={{0,6},{1,7},{2,4},{3,5},{4,2},{5,3},{6,0},{7,1},{8,14},{9,15},{10,... | collective-permute-start | bytes 5898248 | tf_op jit(solution)/shard_map/ppermute | solution.py:371
  965.5 119.6 %collective-permute-start.30 = (bf16[512,1920]{1,0:T(8,128)(2,1)}, bf16[512,1920]{1,0:T(8,128)(2,1)}, u32[]{:S(2)}, u32[]{:S(2)}) collective-permute-start(bf16[512,1920]{1,0:T(8,128)(2,1)} %get-tuple-element.74), channel_id=1, source_target_pairs={{0,7},{1,6},{2,5},{3,4},{4,3},{5,2},{6,1},{7,0},{8,15},{9,14},{10,... | collective-permute-start | bytes 5898248 | tf_op jit(solution)/shard_map/ppermute | solution.py:371
  966.8 162.1 %collective-permute-start.31 = (bf16[512,1920]{1,0:T(8,128)(2,1)}, bf16[512,1920]{1,0:T(8,128)(2,1)}, u32[]{:S(2)}, u32[]{:S(2)}) collective-permute-start(bf16[512,1920]{1,0:T(8,128)(2,1)} %get-tuple-element.75), channel_id=1, source_target_pairs={{0,10},{1,11},{2,8},{3,9},{4,14},{5,15},{6,12},{7,13},{8,2},{9,3},... | collective-permute-start | bytes 5898248 | tf_op jit(solution)/shard_map/ppermute | solution.py:371
  976.9 431.5 %copy-start.11 = (f32[1536]{0:T(1024)}, f32[1536]{0:T(1024)S(1)}, u32[]{:S(2)}) copy-start(f32[1536]{0:T(1024)S(1)} %reduce_sum.19) | copy-start | bytes 18436
  1058.0 327.2 %collective-permute-start.27 = (bf16[512,1920]{1,0:T(8,128)(2,1)}, bf16[512,1920]{1,0:T(8,128)(2,1)}, u32[]{:S(2)}, u32[]{:S(2)}) collective-permute-start(bf16[512,1920]{1,0:T(8,128)(2,1)} %get-tuple-element.71), channel_id=1, source_target_pairs={{0,14},{1,15},{2,12},{3,13},{4,10},{5,11},{6,8},{7,9},{8,6},{9,7},... | collective-permute-start | bytes 5898248 | tf_op jit(solution)/shard_map/ppermute | solution.py:371
  1060.4 324.8 %collective-permute-start.28 = (bf16[512,1920]{1,0:T(8,128)(2,1)S(1)}, bf16[512,1920]{1,0:T(8,128)(2,1)}, u32[]{:S(2)}, u32[]{:S(2)}) collective-permute-start(bf16[512,1920]{1,0:T(8,128)(2,1)S(1)} %copy-done.4), channel_id=1, source_target_pairs={{0,15},{1,14},{2,13},{3,12},{4,11},{5,10},{6,9},{7,8},{8,7},{9,6},... | collective-permute-start | bytes 5898248 | tf_op jit(solution)/shard_map/ppermute | solution.py:371
  1085.1 210.3 %collective-permute-start.32 = (bf16[512,1920]{1,0:T(8,128)(2,1)}, bf16[512,1920]{1,0:T(8,128)(2,1)}, u32[]{:S(2)}, u32[]{:S(2)}) collective-permute-start(bf16[512,1920]{1,0:T(8,128)(2,1)} %get-tuple-element.76), channel_id=1, source_target_pairs={{0,11},{1,10},{2,9},{3,8},{4,15},{5,14},{6,13},{7,12},{8,3},{9,2},... | collective-permute-start | bytes 5898248 | tf_op jit(solution)/shard_map/ppermute | solution.py:371
  1128.9 168.2 %collective-permute-start.33 = (bf16[512,1920]{1,0:T(8,128)(2,1)}, bf16[512,1920]{1,0:T(8,128)(2,1)}, u32[]{:S(2)}, u32[]{:S(2)}) collective-permute-start(bf16[512,1920]{1,0:T(8,128)(2,1)} %get-tuple-element.77), channel_id=1, source_target_pairs={{0,12},{1,13},{2,14},{3,15},{4,8},{5,9},{6,10},{7,11},{8,4},{9,5},... | collective-permute-start | bytes 5898248 | tf_op jit(solution)/shard_map/ppermute | solution.py:371
  1130.0 209.1 %collective-permute-start.34 = (bf16[512,1920]{1,0:T(8,128)(2,1)}, bf16[512,1920]{1,0:T(8,128)(2,1)}, u32[]{:S(2)}, u32[]{:S(2)}) collective-permute-start(bf16[512,1920]{1,0:T(8,128)(2,1)} %get-tuple-element.78), channel_id=1, source_target_pairs={{0,13},{1,12},{2,15},{3,14},{4,9},{5,8},{6,11},{7,10},{8,5},{9,4},... | collective-permute-start | bytes 5898248 | tf_op jit(solution)/shard_map/ppermute | solution.py:371
  (24 other events, 226.2 us)
Sparse Core Ops, SparseCore 0:
  10.2 218.9 all-gather.5
  540.8 103.4 all-gather.7
  944.7 30.5 all-gather.9
